TPU v7x, 32 devices: a whole 2x2x4 slice. The times are simulated.
32 devices in a mesh: dp: 4 (over z), blk: 4 (over y, core), aa: 2 (over x).
Axes of the slice: x: 2, y: 2, z: 4, core: 2. Of those that a mesh axis runs over, the one named last changes fastest.
Arguments:
- queries: bfloat16 [4, 1024, 2048], P('dp', ('blk', 'aa')), may hold values from -128 to 128
- keys: bfloat16 [4, 1024, 512], P('dp', ('blk', 'aa')), may hold values from -10 to 10
- values: bfloat16 [4, 1024, 512], P('dp', ('blk', 'aa')), may hold values from -6 to 6
- grad_parts: float32 [4, 8, 131072], P('dp', ('blk', 'aa')), may hold values from -192 to 192
Outputs:
- attended: bfloat16 [4, 1024, 2048], P('dp', 'blk', 'aa')
- grad_mean: float32 [131072], P(('blk', 'aa'))
All inputs are finite; a program needn't handle non-finite values.
Results may differ from a plain program's by a relative error of at most 0.008.
Values may be sent and summed in bfloat16 or wider, within the bound.
A program may use at most 64 MiB of HBM per device.

v0:
```python
import jax
import jax.numpy as jnp
from jax import lax
from jax.sharding import PartitionSpec as P

HQ = 16
KVH = 4
DH = 128


def shifted(value, axis, by):
    peers = lax.axis_size(axis)
    pairs = [(i, i + by) for i in range(peers) if 0 <= i + by < peers]
    return lax.ppermute(value, axis, pairs)


def attend(queries, keys, values):
    rows = queries.shape[0]
    size_aa = lax.axis_size("aa")
    spread = max(KVH, size_aa)
    q_heads = queries.reshape(rows, HQ, DH)
    k_heads = jnp.repeat(keys.reshape(rows, KVH, DH), spread // KVH, axis=1)
    v_heads = jnp.repeat(values.reshape(rows, KVH, DH), spread // KVH, axis=1)
    q_here, k_here, v_here = (
        lax.all_to_all(q_heads, "aa", split_axis=1, concat_axis=0, tiled=True),
        lax.all_to_all(k_heads, "aa", split_axis=1, concat_axis=0, tiled=True),
        lax.all_to_all(v_heads, "aa", split_axis=1, concat_axis=0, tiled=True),
    )
    span = q_here.shape[0]
    reach = span // 4
    prior_k, prior_v = shifted((k_here[span - reach :], v_here[span - reach :]), "blk", 1)
    group = q_here.shape[1] // k_here.shape[1]
    k_all = jnp.repeat(jnp.concatenate([prior_k, k_here], 0), group, axis=1)
    v_all = jnp.repeat(jnp.concatenate([prior_v, v_here], 0), group, axis=1)
    step_rows = min(256, reach)
    anchor = lax.axis_index("blk") * span
    scale = DH ** (-0.5)

    def one_block(index):
        offset = index * step_rows
        q_block = lax.dynamic_slice_in_dim(q_here, offset, step_rows, 0)
        k_block = lax.dynamic_slice_in_dim(k_all, offset, step_rows + reach, 0)
        v_block = lax.dynamic_slice_in_dim(v_all, offset, step_rows + reach, 0)
        scores = (
            jnp.einsum("qhd,khd->hqk", q_block, k_block, preferred_element_type=jnp.float32) * scale
        )
        q_pos = anchor + offset + jnp.arange(step_rows, dtype=jnp.int32)
        k_pos = anchor + offset - reach + jnp.arange(step_rows + reach, dtype=jnp.int32)
        allowed = (k_pos[None, :] <= q_pos[:, None]) & (k_pos[None, :] > q_pos[:, None] - reach)
        scores = jnp.where(allowed[None], scores, -1e30)
        top = jnp.max(scores, axis=-1, keepdims=True)
        expo = jnp.exp(scores - top)
        weights = (expo / jnp.sum(expo, axis=-1, keepdims=True)).astype(jnp.bfloat16)
        out = jnp.einsum("hqk,khd->qhd", weights, v_block, preferred_element_type=jnp.float32)
        return out.astype(jnp.bfloat16)

    blocks = lax.map(one_block, jnp.arange(span // step_rows, dtype=jnp.int32))
    return blocks.reshape(span, -1)


def average(grad_parts):
    members = lax.axis_size("blk") * lax.axis_size("aa")
    replicas = lax.axis_size("dp")
    flat_grad = grad_parts.reshape(-1)
    share = lax.psum_scatter(flat_grad, ("blk", "aa"), scatter_dimension=0, tiled=True)
    total = lax.psum(share, "dp")
    return total / (members * replicas)


def shards(queries, keys, values, grad_parts):
    attended = attend(queries[0], keys[0], values[0])[None]
    grad_mean = average(grad_parts)
    return (attended, grad_mean)


def solution(mesh):
    placed = (
        P("dp", ("blk", "aa"), None),
        P("dp", ("blk", "aa"), None),
        P("dp", ("blk", "aa"), None),
        P("dp", ("blk", "aa"), None),
    )
    return jax.shard_map(
        shards,
        mesh=mesh,
        in_specs=placed,
        out_specs=(P("dp", "blk", "aa"), P(("blk", "aa"))),
        check_vma=False,
    )
```

profile of v0, /device:TPU:0, one launch (start us, length us, event | category | flops | bytes accessed | tf_op | source)
XLA Modules:
  0.0 135.1 jit_solution(9205147777204657953)
XLA Ops:
  7.2 1.0 copy.38
  8.2 0.8 copy.39
  9.0 4.4 %all-to-all-start.2 = ((bf16[128,4,128]{2,0,1:T(8,128)(2,1)}), bf16[128,4,128]{2,0,1:T(8,128)(2,1)S(1)}, u32[]{:S(2)}, u32[]{:S(2)}) async-start(bf16[128,4,128]{2,0,1:T(8,128)(2,1)} %copy.39), calls=%async_computation.2 | async-start | bytes 262144 | tf_op jit(solution)/shard_map/all_to_all | solution.py:26
  13.3 0.1 copy.31
  13.5 0.8 copy.32
  14.2 3.7 %all-to-all-done.2 = bf16[128,4,128]{2,0,1:T(8,128)(2,1)S(1)} async-done(((bf16[128,4,128]{2,0,1:T(8,128)(2,1)}), bf16[128,4,128]{2,0,1:T(8,128)(2,1)S(1)}, u32[]{:S(2)}, u32[]{:S(2)}) %all-to-all-start.2) | async-done | bytes 131104 | tf_op jit(solution)/shard_map/all_to_all | solution.py:26
  17.9 3.4 %all-to-all-start = ((bf16[128,4,128]{2,0,1:T(8,128)(2,1)}), bf16[128,4,128]{2,0,1:T(8,128)(2,1)S(1)}, u32[]{:S(2)}, u32[]{:S(2)}) async-start(bf16[128,4,128]{2,0,1:T(8,128)(2,1)} %copy.32), calls=%async_computation | async-start | bytes 262144 | tf_op jit(solution)/shard_map/all_to_all | solution.py:27
  21.3 1.3 collective-permute-start.1
  22.6 0.3 copy.34
  22.9 1.0 copy.35
  23.9 1.8 %all-to-all-done = bf16[128,4,128]{2,0,1:T(8,128)(2,1)S(1)} async-done(((bf16[128,4,128]{2,0,1:T(8,128)(2,1)}), bf16[128,4,128]{2,0,1:T(8,128)(2,1)S(1)}, u32[]{:S(2)}, u32[]{:S(2)}) %all-to-all-start) | async-done | bytes 131104 | tf_op jit(solution)/shard_map/all_to_all | solution.py:27
  25.7 3.5 %all-to-all-start.1 = ((bf16[128,16,128]{2,0,1:T(8,128)(2,1)}), bf16[128,16,128]{2,0,1:T(8,128)(2,1)S(1)}, u32[]{:S(2)}, u32[]{:S(2)}) async-start(bf16[128,16,128]{2,0,1:T(8,128)(2,1)} %copy.35), calls=%async_computation.1 | async-start | bytes 1048576 | tf_op jit(solution)/shard_map/all_to_all | solution.py:25
  29.2 0.0 all-reduce.6.cloned.1.call-start
  29.3 0.7 all-reduce.6.cloned.1.call-update
  30.0 0.6 copy-done.2
  30.7 0.6 dynamic-slice
  32.0 2.9 %collective-permute-start = (bf16[64,2,128]{2,0,1:T(8,128)(2,1)S(1)}, bf16[64,2,128]{2,0,1:T(8,128)(2,1)S(1)}, u32[]{:S(2)}, u32[]{:S(2)}) collective-permute-start(bf16[64,2,128]{2,0,1:T(8,128)(2,1)S(1)} %slice.8), channel_id=1, source_target_pairs={{0,2},{2,4},{4,6},{1,3},{3,5},{5,7},{8,10},{10,12},{12,14},{9,11},... | collective-permute-start | bytes 98312 | tf_op jit(solution)/shard_map/ppermute | solution.py:14
  34.9 0.8 collective-permute-done
  35.7 2.7 %all-to-all-done.1 = bf16[128,16,128]{2,0,1:T(8,128)(2,1)S(1)} async-done(((bf16[128,16,128]{2,0,1:T(8,128)(2,1)}), bf16[128,16,128]{2,0,1:T(8,128)(2,1)S(1)}, u32[]{:S(2)}, u32[]{:S(2)}) %all-to-all-start.1) | async-done | bytes 524320 | tf_op jit(solution)/shard_map/all_to_all | solution.py:25
  38.4 0.3 copy.37
  38.7 51.6 %all-reduce.6.cloned.1.call-done = f32[131072]{0:T(1024)} async-done(((f32[131072]{0:T(1024)}), f32[131072]{0:T(1024)}) %all-reduce.6.cloned.1.call-update) | async-done | bytes 524304
  90.3 1.5 %dynamic-slice.1 = f32[16384]{0:T(1024)} dynamic-slice(f32[131072]{0:T(1024)} %all-reduce.6.cloned.1.call-done, u32[]{:T(128)S(6)} %multiply.2), dynamic_slice_sizes={16384} | dynamic-slice | bytes 131076
  91.8 0.1 broadcast_in_dim.47
  91.8 0.1 broadcast_in_dim.46
  91.9 9.1 %while.13 = (s32[]{:T(128)}, bf16[4,64,8,128]{3,2,1,0:T(8,128)(2,1)S(1)}, s32[4]{0:T(128)S(1)}, bf16[320,8,128]{2,0,1:T(8,128)(2,1)S(1)}, s32[]{:T(128)}, /*inde...) while((s32[]{:T(128)}, ...), condition=%wide.region_3.4_spmd, body=%wide.region_0.3_spmd.sunk | while | flops 34038152 | bytes 1859840 | solution.py:57
  92.0 0.6 dynamic_slice.47
  93.2 0.1 compare_and_fusion.2
  93.4 0.5 fusion.37
  93.8 0.3 fusion.38
  94.1 0.1 copy_dynamic-update-slice_fusion.2
  94.2 0.6 dynamic_slice.47
  95.5 0.1 compare_and_fusion.2
  95.6 0.5 fusion.37
  96.1 0.3 fusion.38
  96.4 0.1 copy_dynamic-update-slice_fusion.2
  96.5 0.6 dynamic_slice.47
  97.8 0.1 compare_and_fusion.2
  97.9 0.5 fusion.37
  98.4 0.3 fusion.38
  98.6 0.1 copy_dynamic-update-slice_fusion.2
  98.8 0.6 dynamic_slice.47
  100.0 0.1 compare_and_fusion.2
  100.2 0.5 fusion.37
  100.6 0.3 fusion.38
  100.9 0.1 copy_dynamic-update-slice_fusion.2
  101.0 1.0 broadcast_in_dim_reshape.3
  102.0 24.8 %all-reduce.4.cloned.1.call-done = f32[16384]{0:T(1024)} async-done(((f32[16384]{0:T(1024)}), f32[16384]{0:T(1024)}) %all-reduce.4.cloned.1.call-update) | async-done | bytes 65552 | tf_op jit(solution)/shard_map/psum | solution.py:66
  126.8 1.5 %broadcast_multiply_fusion = f32[16384]{0:T(1024)} fusion(f32[16384]{0:T(1024)} %all-reduce.4.cloned.1.call-done), kind=kLoop, calls=%fused_computation.26 | loop fusion | flops 16384 | bytes 131072 | tf_op jit(solution)/shard_map/div | solution.py:67
  (28 shorter events, 0.2 us)
Async XLA Ops:
  9.0 4.4 %copy-start.1 = (bf16[1,128,512]{2,1,0:T(8,128)(2,1)S(1)}, bf16[1,128,512]{2,1,0:T(8,128)(2,1)}, u32[]{:S(2)}) copy-start(bf16[1,128,512]{2,1,0:T(8,128)(2,1)} %param.8) | copy-start | bytes 393220
  9.0 8.9 %all-to-all-start.2 = ((bf16[128,4,128]{2,0,1:T(8,128)(2,1)}), bf16[128,4,128]{2,0,1:T(8,128)(2,1)S(1)}, u32[]{:S(2)}, u32[]{:S(2)}) async-start(bf16[128,4,128]{2,0,1:T(8,128)(2,1)} %copy.39), calls=%async_computation.2 | async-start | bytes 262144 | tf_op jit(solution)/shard_map/all_to_all | solution.py:26
  13.3 9.3 %copy-start = (bf16[1,128,2048]{2,1,0:T(8,128)(2,1)S(1)}, bf16[1,128,2048]{2,1,0:T(8,128)(2,1)}, u32[]{:S(2)}) copy-start(bf16[1,128,2048]{2,1,0:T(8,128)(2,1)} %param.6) | copy-start | bytes 1572868
  17.9 7.8 %all-to-all-start = ((bf16[128,4,128]{2,0,1:T(8,128)(2,1)}), bf16[128,4,128]{2,0,1:T(8,128)(2,1)S(1)}, u32[]{:S(2)}, u32[]{:S(2)}) async-start(bf16[128,4,128]{2,0,1:T(8,128)(2,1)} %copy.32), calls=%async_computation | async-start | bytes 262144 | tf_op jit(solution)/shard_map/all_to_all | solution.py:27
  21.3 13.5 %collective-permute-start.1 = (bf16[64,2,128]{2,0,1:T(8,128)(2,1)S(1)}, bf16[64,2,128]{2,0,1:T(8,128)(2,1)S(1)}, u32[]{:S(2)}, u32[]{:S(2)}) collective-permute-start(bf16[64,2,128]{2,0,1:T(8,128)(2,1)S(1)} %slice.9), channel_id=1, source_target_pairs={{0,2},{2,4},{4,6},{1,3},{3,5},{5,7},{8,10},{10,12},{12,14},{9,11},... | collective-permute-start | bytes 98312 | tf_op jit(solution)/shard_map/ppermute | solution.py:14
  25.7 12.6 %all-to-all-start.1 = ((bf16[128,16,128]{2,0,1:T(8,128)(2,1)}), bf16[128,16,128]{2,0,1:T(8,128)(2,1)S(1)}, u32[]{:S(2)}, u32[]{:S(2)}) async-start(bf16[128,16,128]{2,0,1:T(8,128)(2,1)} %copy.35), calls=%async_computation.1 | async-start | bytes 1048576 | tf_op jit(solution)/shard_map/all_to_all | solution.py:25
  29.2 61.0 %all-reduce.6.cloned.1.call-start = ((), (), s32[]{:S(2)}) async-start(), calls=%async_computation.4 | async-start | bytes 1048576
  30.0 96.8 %all-reduce.4.cloned.1.call-start = ((), (), s32[]{:S(2)}) async-start(), calls=%async_computation.3 | async-start | bytes 131072 | tf_op jit(solution)/shard_map/psum | solution.py:66
  30.0 0.7 copy-start.2
  32.0 3.7 %collective-permute-start = (bf16[64,2,128]{2,0,1:T(8,128)(2,1)S(1)}, bf16[64,2,128]{2,0,1:T(8,128)(2,1)S(1)}, u32[]{:S(2)}, u32[]{:S(2)}) collective-permute-start(bf16[64,2,128]{2,0,1:T(8,128)(2,1)S(1)} %slice.8), channel_id=1, source_target_pairs={{0,2},{2,4},{4,6},{1,3},{3,5},{5,7},{8,10},{10,12},{12,14},{9,11},... | collective-permute-start | bytes 98312 | tf_op jit(solution)/shard_map/ppermute | solution.py:14
Sparse Core Ops, SparseCore 0:
  33.1 57.0 all-reduce.5
  93.1 33.6 all-reduce.3
where the time goes:
time: 136 us; the launch traced here: 135 us
  waiting for transfers between devices  86 us (63%)
  starting transfers between devices  15.5 us (11%)
  between operations  14.9 us (11%)
  local copies, waits for them, and re-layouts  11.1 us (8%)
  loops' own time  2.97 us (2%)
  matrix products  2.88 us (2%)
  other arithmetic  1.87 us (1%)
    unnamed x3, waiting for transfers between devices  52.3 us
    psum x1, waiting for transfers between devices, average(): total = lax.psum(share, 'dp')  24.8 us
    all_to_all x1, starting transfers between devices, attend(): lax.all_to_all(k_heads, 'aa', split_axis=1, concat_axis=0, tiled=True)  4.37 us
    ppermute x2, starting transfers between devices, shifted(): return lax.ppermute(value, axis, pairs)  4.15 us
    unnamed x11, local copies, waits for them, and re-layouts  4.12 us
    all_to_all x1, waiting for transfers between devices, attend(): lax.all_to_all(k_heads, 'aa', split_axis=1, concat_axis=0, tiled=True)  3.66 us
    all_to_all x1, starting transfers between devices, attend(): lax.all_to_all(q_heads, 'aa', split_axis=1, concat_axis=0, tiled=True)  3.49 us
    all_to_all x1, starting transfers between devices, attend(): lax.all_to_all(v_heads, 'aa', split_axis=1, concat_axis=0, tiled=True)  3.38 us
  transfers between devices with their start and end apart: 7, of which 6 were waited for; matrix products, arithmetic and copies ran while one was open for 8% of the time, Pallas kernels for 0%

commit v1 on v0

--- a/solution.py
+++ b/solution.py
@@ -63,7 +63,8 @@
     replicas = lax.axis_size("dp")
     flat_grad = grad_parts.reshape(-1)
     share = lax.psum_scatter(flat_grad, ("blk", "aa"), scatter_dimension=0, tiled=True)
-    total = lax.psum(share, "dp")
+    terms = lax.all_gather(share, "dp", axis=0, tiled=False)
+    total = terms.sum(axis=0)
     return total / (members * replicas)
 
 

time: 136 us -> 113 us (0.83)
  waiting for transfers between devices: 86 us -> 51 us
  blocking collectives: 0 us -> 13.9 us
    psum x1 -> x0, waiting for transfers between devices: 24.8 us -> none  [average(): total = lax.psum(share, 'dp')]
    all_gather x0 -> x1, blocking collectives: none -> 13.9 us  [average(): terms = lax.all_gather(share, 'dp', axis=0, tiled=False)]
    unnamed x3 -> x2, waiting for transfers between devices: 52.3 us -> 42 us
    unnamed x11 -> x12, local copies, waits for them, and re-layouts: 4.12 us -> 3.51 us
  transfers between devices with their start and end apart: 7 -> 6, of which waited for: 6 -> 5; matrix products, arithmetic and copies ran while one was open for 8% -> 9% of each run, Pallas kernels for 0% -> 0%
where the time goes in v1:
time: 113 us
  waiting for transfers between devices  51 us (45%)
  starting transfers between devices  15.4 us (14%)
  between operations  14.9 us (13%)
  blocking collectives  13.9 us (12%)
  local copies, waits for them, and re-layouts  10.6 us (9%)
  loops' own time  2.97 us (3%)
  matrix products  2.87 us (3%)
  other arithmetic  1.19 us (1%)
    unnamed x2, waiting for transfers between devices  42 us
    all_gather x1, blocking collectives, average(): terms = lax.all_gather(share, 'dp', axis=0, tiled=False)  13.9 us
    all_to_all x1, starting transfers between devices, attend(): lax.all_to_all(k_heads, 'aa', split_axis=1, concat_axis=0, tiled=True)  4.37 us
    ppermute x2, starting transfers between devices, shifted(): return lax.ppermute(value, axis, pairs)  4.15 us
    all_to_all x1, waiting for transfers between devices, attend(): lax.all_to_all(k_heads, 'aa', split_axis=1, concat_axis=0, tiled=True)  3.66 us
    unnamed x12, local copies, waits for them, and re-layouts  3.51 us
    all_to_all x1, starting transfers between devices, attend(): lax.all_to_all(q_heads, 'aa', split_axis=1, concat_axis=0, tiled=True)  3.49 us
    all_to_all x1, starting transfers between devices, attend(): lax.all_to_all(v_heads, 'aa', split_axis=1, concat_axis=0, tiled=True)  3.38 us
  transfers between devices with their start and end apart: 6, of which 5 were waited for; matrix products, arithmetic and copies ran while one was open for 9% of the time, Pallas kernels for 0%

profile of v1, /device:TPU:0, one launch (start us, length us, event | category | flops | bytes accessed | tf_op | source)
XLA Modules:
  0.0 112.8 jit_solution(17556771901272356881)
XLA Ops:
  7.2 1.0 copy.50
  8.2 0.8 copy.51
  9.0 4.4 %all-to-all-start.2 = ((bf16[128,4,128]{2,0,1:T(8,128)(2,1)}), bf16[128,4,128]{2,0,1:T(8,128)(2,1)S(1)}, u32[]{:S(2)}, u32[]{:S(2)}) async-start(bf16[128,4,128]{2,0,1:T(8,128)(2,1)} %copy.51), calls=%async_computation.2 | async-start | bytes 262144 | tf_op jit(solution)/shard_map/all_to_all | solution.py:26
  13.3 0.1 copy.43
  13.5 0.8 copy.44
  14.2 3.7 %all-to-all-done.2 = bf16[128,4,128]{2,0,1:T(8,128)(2,1)S(1)} async-done(((bf16[128,4,128]{2,0,1:T(8,128)(2,1)}), bf16[128,4,128]{2,0,1:T(8,128)(2,1)S(1)}, u32[]{:S(2)}, u32[]{:S(2)}) %all-to-all-start.2) | async-done | bytes 131104 | tf_op jit(solution)/shard_map/all_to_all | solution.py:26
  17.9 3.4 %all-to-all-start = ((bf16[128,4,128]{2,0,1:T(8,128)(2,1)}), bf16[128,4,128]{2,0,1:T(8,128)(2,1)S(1)}, u32[]{:S(2)}, u32[]{:S(2)}) async-start(bf16[128,4,128]{2,0,1:T(8,128)(2,1)} %copy.44), calls=%async_computation | async-start | bytes 262144 | tf_op jit(solution)/shard_map/all_to_all | solution.py:27
  21.3 1.3 %collective-permute-start.1 = (bf16[64,2,128]{2,0,1:T(8,128)(2,1)S(1)}, bf16[64,2,128]{2,0,1:T(8,128)(2,1)S(1)}, u32[]{:S(2)}, u32[]{:S(2)}) collective-permute-start(bf16[64,2,128]{2,0,1:T(8,128)(2,1)S(1)} %slice.9), channel_id=1, source_target_pairs={{0,2},{2,4},{4,6},{1,3},{3,5},{5,7},{8,10},{10,12},{12,14},{9,11},... | collective-permute-start | bytes 98312 | tf_op jit(solution)/shard_map/ppermute | solution.py:14
  22.6 0.3 copy.46
  22.9 1.0 copy.47
  23.9 1.8 %all-to-all-done = bf16[128,4,128]{2,0,1:T(8,128)(2,1)S(1)} async-done(((bf16[128,4,128]{2,0,1:T(8,128)(2,1)}), bf16[128,4,128]{2,0,1:T(8,128)(2,1)S(1)}, u32[]{:S(2)}, u32[]{:S(2)}) %all-to-all-start) | async-done | bytes 131104 | tf_op jit(solution)/shard_map/all_to_all | solution.py:27
  25.7 3.5 %all-to-all-start.1 = ((bf16[128,16,128]{2,0,1:T(8,128)(2,1)}), bf16[128,16,128]{2,0,1:T(8,128)(2,1)S(1)}, u32[]{:S(2)}, u32[]{:S(2)}) async-start(bf16[128,16,128]{2,0,1:T(8,128)(2,1)} %copy.47), calls=%async_computation.1 | async-start | bytes 1048576 | tf_op jit(solution)/shard_map/all_to_all | solution.py:25
  29.3 0.7 all-reduce.3.cloned.1.call-update
  30.0 0.6 copy-done.2
  30.6 0.6 dynamic-slice
  31.9 2.9 %collective-permute-start = (bf16[64,2,128]{2,0,1:T(8,128)(2,1)S(1)}, bf16[64,2,128]{2,0,1:T(8,128)(2,1)S(1)}, u32[]{:S(2)}, u32[]{:S(2)}) collective-permute-start(bf16[64,2,128]{2,0,1:T(8,128)(2,1)S(1)} %slice.8), channel_id=1, source_target_pairs={{0,2},{2,4},{4,6},{1,3},{3,5},{5,7},{8,10},{10,12},{12,14},{9,11},... | collective-permute-start | bytes 98312 | tf_op jit(solution)/shard_map/ppermute | solution.py:14
  34.8 0.8 collective-permute-done
  35.7 2.7 %all-to-all-done.1 = bf16[128,16,128]{2,0,1:T(8,128)(2,1)S(1)} async-done(((bf16[128,16,128]{2,0,1:T(8,128)(2,1)}), bf16[128,16,128]{2,0,1:T(8,128)(2,1)S(1)}, u32[]{:S(2)}, u32[]{:S(2)}) %all-to-all-start.1) | async-done | bytes 524320 | tf_op jit(solution)/shard_map/all_to_all | solution.py:25
  38.4 0.3 copy.49
  38.7 0.1 broadcast_in_dim.47
  38.8 0.1 broadcast_in_dim.46
  38.9 9.0 %while.13 = (s32[]{:T(128)}, bf16[4,64,8,128]{3,2,1,0:T(8,128)(2,1)S(1)}, s32[4]{0:T(128)S(1)}, bf16[320,8,128]{2,0,1:T(8,128)(2,1)S(1)}, s32[]{:T(128)}, /*inde...) while((s32[]{:T(128)}, ...), condition=%wide.region_3.4_spmd, body=%wide.region_0.3_spmd.sunk | while | flops 34038152 | bytes 1859840 | solution.py:57
  38.9 0.6 dynamic_slice.47
  40.2 0.1 compare_and_fusion.2
  40.3 0.5 fusion.37
  40.8 0.3 fusion.38
  41.0 0.1 copy_dynamic-update-slice_fusion.2
  41.2 0.6 dynamic_slice.47
  42.4 0.1 compare_and_fusion.2
  42.6 0.5 fusion.37
  43.0 0.3 fusion.38
  43.3 0.1 copy_dynamic-update-slice_fusion.2
  43.4 0.6 dynamic_slice.47
  44.7 0.1 compare_and_fusion.2
  44.8 0.5 fusion.37
  45.3 0.3 fusion.38
  45.6 0.1 copy_dynamic-update-slice_fusion.2
  45.7 0.6 dynamic_slice.47
  47.1 0.5 fusion.37
  47.5 0.3 fusion.38
  47.8 0.1 copy_dynamic-update-slice_fusion.2
  47.9 1.0 broadcast_in_dim_reshape.3
  49.0 41.3 %all-reduce.3.cloned.1.call-done = f32[131072]{0:T(1024)} async-done(((f32[131072]{0:T(1024)}), f32[131072]{0:T(1024)}) %all-reduce.3.cloned.1.call-update) | async-done | bytes 524304
  90.3 0.8 dynamic-slice-done
  91.1 13.9 %all-gather = f32[65536]{0:T(1024)S(1)} all-gather(f32[16384]{0:T(1024)S(1)} %dynamic-slice-done), channel_id=2, replica_groups=mesh['dp'=4,'blk'=4,'aa'=2] {'dp'}, dimensions={0}, use_global_device_ids=true | all-gather | bytes 327680 | tf_op jit(solution)/shard_map/all_gather | solution.py:66
  105.0 0.1 reshape.91
  105.1 0.2 reduce_sum.22
  105.3 0.6 broadcast_multiply_fusion
  (29 shorter events, 0.3 us)
Async XLA Ops:
  9.0 4.4 %copy-start.1 = (bf16[1,128,512]{2,1,0:T(8,128)(2,1)S(1)}, bf16[1,128,512]{2,1,0:T(8,128)(2,1)}, u32[]{:S(2)}) copy-start(bf16[1,128,512]{2,1,0:T(8,128)(2,1)} %param.8) | copy-start | bytes 393220
  9.0 8.9 %all-to-all-start.2 = ((bf16[128,4,128]{2,0,1:T(8,128)(2,1)}), bf16[128,4,128]{2,0,1:T(8,128)(2,1)S(1)}, u32[]{:S(2)}, u32[]{:S(2)}) async-start(bf16[128,4,128]{2,0,1:T(8,128)(2,1)} %copy.51), calls=%async_computation.2 | async-start | bytes 262144 | tf_op jit(solution)/shard_map/all_to_all | solution.py:26
  13.3 9.3 %copy-start = (bf16[1,128,2048]{2,1,0:T(8,128)(2,1)S(1)}, bf16[1,128,2048]{2,1,0:T(8,128)(2,1)}, u32[]{:S(2)}) copy-start(bf16[1,128,2048]{2,1,0:T(8,128)(2,1)} %param.6) | copy-start | bytes 1572868
  17.9 7.8 %all-to-all-start = ((bf16[128,4,128]{2,0,1:T(8,128)(2,1)}), bf16[128,4,128]{2,0,1:T(8,128)(2,1)S(1)}, u32[]{:S(2)}, u32[]{:S(2)}) async-start(bf16[128,4,128]{2,0,1:T(8,128)(2,1)} %copy.44), calls=%async_computation | async-start | bytes 262144 | tf_op jit(solution)/shard_map/all_to_all | solution.py:27
  21.3 13.5 %collective-permute-start.1 = (bf16[64,2,128]{2,0,1:T(8,128)(2,1)S(1)}, bf16[64,2,128]{2,0,1:T(8,128)(2,1)S(1)}, u32[]{:S(2)}, u32[]{:S(2)}) collective-permute-start(bf16[64,2,128]{2,0,1:T(8,128)(2,1)S(1)} %slice.9), channel_id=1, source_target_pairs={{0,2},{2,4},{4,6},{1,3},{3,5},{5,7},{8,10},{10,12},{12,14},{9,11},... | collective-permute-start | bytes 98312 | tf_op jit(solution)/shard_map/ppermute | solution.py:14
  25.7 12.6 %all-to-all-start.1 = ((bf16[128,16,128]{2,0,1:T(8,128)(2,1)}), bf16[128,16,128]{2,0,1:T(8,128)(2,1)S(1)}, u32[]{:S(2)}, u32[]{:S(2)}) async-start(bf16[128,16,128]{2,0,1:T(8,128)(2,1)} %copy.47), calls=%async_computation.1 | async-start | bytes 1048576 | tf_op jit(solution)/shard_map/all_to_all | solution.py:25
  29.2 61.0 %all-reduce.3.cloned.1.call-start = ((), (), s32[]{:S(2)}) async-start(), calls=%async_computation.3 | async-start | bytes 1048576
  30.0 0.7 copy-start.2
  31.9 3.7 %collective-permute-start = (bf16[64,2,128]{2,0,1:T(8,128)(2,1)S(1)}, bf16[64,2,128]{2,0,1:T(8,128)(2,1)S(1)}, u32[]{:S(2)}, u32[]{:S(2)}) collective-permute-start(bf16[64,2,128]{2,0,1:T(8,128)(2,1)S(1)} %slice.8), channel_id=1, source_target_pairs={{0,2},{2,4},{4,6},{1,3},{3,5},{5,7},{8,10},{10,12},{12,14},{9,11},... | collective-permute-start | bytes 98312 | tf_op jit(solution)/shard_map/ppermute | solution.py:14
  90.3 0.8 dynamic-slice-start
Sparse Core Ops, SparseCore 0:
  33.1 57.0 all-reduce.2
